TPU v7x, 32 devices: a whole 2x2x4 slice. The times are simulated.
32 devices in a mesh: prompt: 4 (over z), sample: 4 (over x, core), vocab: 2 (over y).
Axes of the slice: x: 2, y: 2, z: 4, core: 2. Of those that a mesh axis runs over, the one named last changes fastest.
Arguments:
- hidden: bfloat16 [4, 24, 3584], P('sample', ('prompt', 'vocab')), may hold values from -170 to 170
- unembed: bfloat16 [152064, 3584], P(('prompt', 'vocab')), may hold values from -1 to 1
- token_ids: int32 [4, 24], P('sample', ('prompt', 'vocab')), may hold values from 0 to 152063, as said below
- old_logp: float32 [4, 24], P('sample', ('prompt', 'vocab')), may hold values from -14 to -11
- ref_logp: float32 [4, 24], P('sample', ('prompt', 'vocab')), may hold values from -14 to -11
- loss_mask: int32 [4, 24], P('sample', ('prompt', 'vocab')), may hold values 0 or 1
- lengths: int32 [4, 4], P('prompt', 'sample'), may hold values from 1 to 6, as said below
- sample_valid: int32 [4, 4], P('prompt', 'sample'), may hold values 0 or 1
- rewards: int32 [4, 4], P('prompt', 'sample'), may hold values from -300 to 300
Outputs:
- token_logp: float32 [4, 24], P('sample', ('prompt', 'vocab'))
- token_loss: float32 [4, 24], P('sample', ('prompt', 'vocab'))
- advantages: float32 [4, 4], P('prompt', 'sample')
- loss: float32 [], replicated
Inputs may be any that keep to these rules, and one draw needn't show every extreme that they name: `token_ids`: token ids name vocabulary entries. `lengths`: some response in every draw has length 6.
All inputs are finite; a program needn't handle non-finite values. No bound on the sum of `loss_mask` or of `sample_valid` on one device may be relied on, other than what follows from the above.
Results may differ from a plain program's by a relative error of at most 0.0003.
Values may be sent and summed in bfloat16 or wider, within the bound.
A program may use at most 192 MiB of HBM per device.

v0:
```python
import jax
import jax.numpy as jnp
from jax import lax
from jax.sharding import PartitionSpec as P

clip_low = 0.8
clip_high = 1.2
dual_clip = 3.0
kl_weight = 0.04
reward_unit = 0.01
std_floor = 0.5


def combined_all(value, axis, join):
    pieces = jax.tree.map(lambda part: lax.all_gather(part, axis), value)
    head = jax.tree.map(lambda part: part[0], pieces)
    tail = jax.tree.map(lambda part: part[1:], pieces)
    total, _ = lax.scan(lambda total, slab: (join(total, slab), None), head, tail)
    return total


def shard_stats(row_block, labels, weight, vocab_start):
    logits = lax.dot_general(
        row_block, weight, (((1,), (1,)), ((), ())), preferred_element_type=jnp.float32
    )
    local_peak = jnp.max(logits, axis=1)
    exp_total = jnp.sum(jnp.exp(logits - local_peak[:, None]), axis=1)
    column = vocab_start + lax.broadcasted_iota(jnp.int32, logits.shape, 1)
    target = jnp.sum(jnp.where(column == labels[:, None], logits, 0.0), axis=1)
    return (local_peak, exp_total, target)


def merge_pairs(first_part, second_part):
    peak_one, total_one, target_one = first_part
    peak_two, total_two, target_two = second_part
    joined_peak = jnp.maximum(peak_one, peak_two)
    joined_total = total_one * jnp.exp(peak_one - joined_peak) + total_two * jnp.exp(
        peak_two - joined_peak
    )
    return (joined_peak, joined_total, target_one + target_two)


def local(
    hidden, unembed, token_ids, old_logp, ref_logp, loss_mask, lengths, sample_valid, rewards
):
    samples, local_rows, width = hidden.shape
    vocab_rows = unembed.shape[0]
    vocab_start = lax.axis_index(("prompt", "vocab")) * vocab_rows
    positions = lax.axis_index("vocab") * local_rows + lax.broadcasted_iota(
        jnp.int32, (samples, local_rows), 1
    )
    live_rows = (loss_mask == 1) & (positions < lengths.T) & (sample_valid.T == 1)
    live_float = live_rows.astype(jnp.float32)
    valid_f = sample_valid.astype(jnp.float32)
    scores = rewards.astype(jnp.float32) * reward_unit
    group_count, first_moment, second_moment = lax.psum(
        (
            jnp.sum(valid_f, axis=1),
            jnp.sum(valid_f * scores, axis=1),
            jnp.sum(valid_f * scores * scores, axis=1),
        ),
        "sample",
    )
    safe_count = jnp.maximum(group_count, 1.0)
    group_mean = first_moment / safe_count
    spread = jnp.sqrt(jnp.maximum(second_moment / safe_count - group_mean * group_mean, 0.0))
    advantages = valid_f * (scores - group_mean[:, None]) / jnp.maximum(spread, std_floor)[:, None]
    part_hidden = lax.all_gather(hidden, ("prompt", "vocab"), axis=1, tiled=True)
    part_ids = lax.all_gather(token_ids, ("prompt", "vocab"), axis=1, tiled=True)
    piece_rows = part_hidden.shape[1]
    piece_stats = shard_stats(
        part_hidden.reshape(samples * piece_rows, width),
        part_ids.reshape(samples * piece_rows),
        unembed,
        vocab_start,
    )
    peak_new = piece_stats[0].reshape(samples, piece_rows)
    total_new = piece_stats[1].reshape(samples, piece_rows)
    target_new = piece_stats[2].reshape(samples, piece_rows)
    row_top, total_all, target_all = combined_all(
        (peak_new, total_new, target_new), ("prompt", "vocab"), merge_pairs
    )
    own_start = lax.axis_index(("prompt", "vocab")) * local_rows

    def own_rows(values):
        return lax.dynamic_slice_in_dim(values, own_start, local_rows, 1)

    raw_logp = own_rows(target_all) - (own_rows(row_top) + jnp.log(own_rows(total_all)))
    token_logp = jnp.where(live_rows, raw_logp, 0.0)
    adv_rows = advantages.T
    prob_ratio = jnp.exp(raw_logp - old_logp)
    gain_side = adv_rows * jnp.minimum(prob_ratio, clip_high)
    loss_side = jnp.maximum(adv_rows * jnp.maximum(prob_ratio, clip_low), dual_clip * adv_rows)
    objective = jnp.where(adv_rows >= 0.0, gain_side, loss_side)
    log_gap = ref_logp - raw_logp
    kl_term = jnp.exp(log_gap) - log_gap - 1.0
    token_loss = jnp.where(live_rows, kl_weight * kl_term - objective, 0.0)
    loss_part = jnp.sum(token_loss)
    loss_total, live_total = lax.psum(
        (loss_part, jnp.sum(live_float)), ("prompt", "sample", "vocab")
    )
    loss = loss_total / jnp.maximum(live_total, 1.0)
    return (token_logp, token_loss, advantages, loss)


def solution(mesh):
    in_specs = (
        P("sample", ("prompt", "vocab"), None),
        P(("prompt", "vocab"), None),
        P("sample", ("prompt", "vocab")),
        P("sample", ("prompt", "vocab")),
        P("sample", ("prompt", "vocab")),
        P("sample", ("prompt", "vocab")),
        P("prompt", "sample"),
        P("prompt", "sample"),
        P("prompt", "sample"),
    )
    out_specs = (
        P("sample", ("prompt", "vocab")),
        P("sample", ("prompt", "vocab")),
        P("prompt", "sample"),
        P(),
    )
    return jax.shard_map(local, mesh=mesh, in_specs=in_specs, out_specs=out_specs, check_vma=False)
```

profile of v0, /device:TPU:0, one launch (start us, length us, event | category | flops | bytes accessed | tf_op | source)
XLA Modules:
  0.0 173.1 jit_solution(1254609279268593562)
XLA Ops:
  1.9 1.3 convert_reduce_fusion
  3.9 10.5 %all-reduce.6 = (f32[1]{0:T(128)}, f32[1]{0:T(128)}, f32[1]{0:T(128)}) all-reduce(f32[1]{0:T(128)} %bitcast.11, f32[1]{0:T(128)} %bitcast.12, f32[1]{0:T(128)} %bitcast.14), channel_id=1, replica_groups=mesh['prompt'=4,'sample'=4,'vocab'=2] {'sample'}, use_global_device_ids=true, to_apply=%region_5.0 | all-reduce | flops 3 | bytes 24 | tf_op jit(solution)/shard_map/psum | solution.py:56
  16.5 0.8 copy.14
  17.3 31.5 %all_gather.15 = bf16[1,24,3584]{2,0,1:T(2,128)(2,1)S(1)} all-gather(bf16[1,3,3584]{2,0,1:T(2,128)(2,1)S(1)} %copy.14), channel_id=1, replica_groups=mesh['prompt'=4,'sample'=4,'vocab'=2] {'prompt','vocab'}, dimensions={1}, use_global_device_ids=true | all-gather | bytes 193536 | tf_op jit(solution)/shard_map/all_gather | solution.py:68
  48.8 0.0 copy-start.3
  48.8 0.0 copy-start.2
  48.8 48.0 %fusion.21 = (f32[24]{0:T(128)S(1)}, f32[24,19008]{1,0:T(8,128)S(1)}) fusion(bf16[19008,3584]{1,0:T(8,128)(2,1)} %param.12, bf16[1,24,3584]{2,0,1:T(2,128)(2,1)S(1)} %all_gather.15), kind=kOutput, calls=%fused_computation.36 | convolution fusion | flops 3270440448 | bytes 138246240 | tf_op jit(solution)/shard_map/dot_general | solution.py:23
  96.8 0.0 copy-start
  96.8 0.0 copy-start.1
  96.8 0.0 copy-done.3
  96.8 0.6 dynamic-slice
  98.1 0.2 dynamic-update-slice
  99.0 0.0 copy-done.2
  99.0 0.1 bitcast_dynamic-update-slice_fusion
  99.1 10.6 %all-reduce.2 = s32[24]{0:T(128)S(1)} all-reduce(s32[24]{0:T(128)S(1)} %bitcast_dynamic-update-slice_fusion), channel_id=1, replica_groups=mesh['prompt'=4,'sample'=4,'vocab'=2] {'prompt','vocab'}, use_global_device_ids=true, to_apply=%add.2 | all-reduce | flops 24 | bytes 192
  109.6 0.7 select_reduce_fusion
  110.4 0.2 dynamic-update-slice.1
  110.6 0.2 dynamic-update-slice.3
  110.8 19.1 %all-reduce.5 = (f32[192]{0:T(256)S(1)}, f32[192]{0:T(256)S(1)}, f32[192]{0:T(256)S(1)}) all-reduce(f32[192]{0:T(256)S(1)} %dynamic-update-slice, f32[192]{0:T(256)S(1)} %dynamic-update-slice.1, f32[192]{0:T(256)S(1)} %dynamic-update-slice.3), channel_id=2, replica_groups=mesh['prompt'=4,'sample'=4,'vocab'=2] {'prompt','vocab'}, use_global_device_ids=true, to_apply=%add | all-reduce | flops 576 | bytes 4608
  129.9 0.1 slice.27
  130.0 0.1 reshape.48
  130.1 0.1 slice.28
  130.2 0.1 reshape.49
  130.3 0.1 slice.29
  130.3 0.1 reshape.50
  130.4 0.3 while.14
  130.7 0.0 copy-done
  130.7 0.0 copy-done.1
  130.7 1.2 fusion.18
  131.9 0.5 broadcast_select_fusion.1
  132.4 37.1 %all-reduce.4 = (f32[]{:T(128)}, f32[]{:T(128)}) all-reduce(f32[]{:T(128)} %get-tuple-element.74, f32[]{:T(128)} %get-tuple-element.72), channel_id=1, replica_groups=mesh['prompt'=4,'sample'=4,'vocab'=2] {'prompt','sample','vocab'}, use_global_device_ids=true, to_apply=%region_9.10 | all-reduce | flops 2 | bytes 16 | tf_op jit(solution)/shard_map/psum | solution.py:99
  (14 shorter events, 0.2 us)
Async XLA Ops:
  48.8 48.0 %copy-start.3 = (u32[32]{0:T(128)S(1)}, u32[32]{0:T(128)}, u32[]{:S(2)}) copy-start(u32[32]{0:T(128)} %constant.69) | copy-start | bytes 388
  48.8 50.2 %copy-start.2 = (s32[1,3]{1,0:T(1,128)S(1)}, s32[1,3]{1,0:T(1,128)}, u32[]{:S(2)}) copy-start(s32[1,3]{1,0:T(1,128)} %param.13) | copy-start | bytes 40
  96.8 33.9 %copy-start = (f32[1,3]{1,0:T(1,128)S(1)}, f32[1,3]{1,0:T(1,128)}, u32[]{:S(2)}) copy-start(f32[1,3]{1,0:T(1,128)} %param.14) | copy-start | bytes 40
  96.8 33.9 %copy-start.1 = (f32[1,3]{1,0:T(1,128)S(1)}, f32[1,3]{1,0:T(1,128)}, u32[]{:S(2)}) copy-start(f32[1,3]{1,0:T(1,128)} %param.15) | copy-start | bytes 40
where the time goes:
time: 174 us; the launch traced here: 173 us
  blocking collectives  109 us (63%)
  matrix products  48 us (28%)
  between operations  9.57 us (6%)
  other arithmetic  3.97 us (2%)
  local copies, waits for them, and re-layouts  2.71 us (2%)
    dot_general x1, matrix products, shard_stats(): lax.dot_general(row_block, weight, (((1,), (1,)), ((), ())), preferred_el...  48 us
    psum x1, blocking collectives, local(): lax.psum((loss_part, jnp.sum(live_float)), ('prompt', 'sample', 'vocab'))  37.1 us
    all_gather x1, blocking collectives, local(): lax.all_gather(hidden, ('prompt', 'vocab'), axis=1, tiled=True)  31.5 us
    unnamed x2, blocking collectives  29.7 us
    psum x1, blocking collectives, local(): lax.psum((jnp.sum(valid_f, axis=1), jnp.sum(valid_f * scores, axis=1), jn...  10.5 us

commit v1 on v0

--- a/solution.py
+++ b/solution.py
@@ -1,6 +1,10 @@
+import functools
+
 import jax
 import jax.numpy as jnp
 from jax import lax
+from jax.experimental import pallas as pl
+from jax.experimental.pallas import tpu as pltpu
 from jax.sharding import PartitionSpec as P
 
 clip_low = 0.8
@@ -40,7 +44,7 @@
     return (joined_peak, joined_total, target_one + target_two)
 
 
-def local(
+def local_plain(
     hidden, unembed, token_ids, old_logp, ref_logp, loss_mask, lengths, sample_valid, rewards
 ):
     samples, local_rows, width = hidden.shape
@@ -103,6 +107,321 @@
     return (token_logp, token_loss, advantages, loss)
 
 
+lanes = 128
+tile_rows = 16
+MESH = pl.DeviceIdType.MESH
+
+
+def chunk_bounds(width):
+    step = 512
+    first = step if width % step == 0 else width
+    bounds = [(0, first)]
+    while bounds[-1][1] < width:
+        start = bounds[-1][1]
+        bounds.append((start, min(start + 2 * step, width)))
+    return bounds
+
+
+def row_blocks(rows):
+    for count in (9, 8, 10, 12, 6, 4, 3, 2, 1):
+        if rows % count == 0 and (rows // count) % tile_rows == 0:
+            return count
+    return 0
+
+
+def merge_slots(tiles):
+    peak = functools.reduce(jnp.maximum, [tile[0:1] for tile in tiles])
+    total = sum(tile[1:2] * jnp.exp(tile[0:1] - peak) for tile in tiles)
+    target = sum(tile[2:3] for tile in tiles)
+    return peak, total, target
+
+
+def fused_kernel(
+    dims, hid, weight, ids, old, ref, mask, lengths, valid, rewards,
+    logp_out, loss_out, adv_out, mean_out,
+    wbuf, zrows, wide, held, acc, fz, fx, fc, sz, sx, sc,
+    wsem, zs, zr, xs, xr, cs, cr, fzs, fzr, fxs, fxr, fcs, fcr, szs, szr, sxs, sxr, scs, scr,
+):
+    np_, ns, nv, local_rows, slot_rows, sub, width, blocks = dims
+    hi_count = ns // 2
+    bounds = chunk_bounds(width)
+    z = lax.axis_index("prompt")
+    s = lax.axis_index("sample")
+    y = lax.axis_index("vocab")
+    hi, lo = s // 2, s % 2
+    block_rows = sub // blocks
+
+    w_start = pl.multiple_of(s * sub, tile_rows)
+    w_copies = []
+    for b in range(blocks):
+        copy = pltpu.make_async_copy(
+            weight.at[pl.ds(w_start + b * block_rows, block_rows), :],
+            wbuf.at[pl.ds(b * block_rows, block_rows), :],
+            wsem.at[b],
+        )
+        copy.start()
+        w_copies.append(copy)
+
+    z_peers = [(lax.rem(z + j, np_), s, y) for j in range(1, np_)]
+    plane = [(a, b) for a in range(hi_count) for b in range(nv) if (a, b) != (0, 0)]
+    x_peers = [(z, lax.rem(hi + a, hi_count) * 2 + lo, lax.rem(y + b, nv)) for a, b in plane]
+    c_peer = (z, hi * 2 + (1 - lo), y)
+    barrier = pltpu.get_barrier_semaphore()
+    peers = z_peers + x_peers + [c_peer]
+    for peer in peers:
+        pl.semaphore_signal(barrier, inc=1, device_id=peer, device_id_type=MESH)
+
+    half = hi_count * nv
+    group_own = hi * nv + y
+    group = lo * half + group_own
+    base_lane = group * tile_rows + z * slot_rows
+
+    lane = lax.broadcasted_iota(jnp.int32, (8, lanes), 1)
+    field = lax.broadcasted_iota(jnp.int32, (8, lanes), 0)
+    valid_s = valid[0, 0]
+    valid_f = valid_s.astype(jnp.float32)
+    score = rewards[0, 0].astype(jnp.float32) * reward_unit
+    inside = (lane >= base_lane) & (lane < base_lane + slot_rows)
+    tile = jnp.where(inside & (field == 4), valid_f, 0.0)
+    tile = jnp.where(inside & (field == 5), score, tile)
+    for r in range(local_rows):
+        here = lane == base_lane + r
+        is_live = (
+            (mask[0, r] == 1) & (y * local_rows + r < lengths[0, 0]) & (valid_s == 1)
+        )
+        live = jnp.where(is_live, 1.0, 0.0)
+        tile = jnp.where(here & (field == 0), ids[0, r].astype(jnp.float32), tile)
+        tile = jnp.where(here & (field == 1), old[0, r], tile)
+        tile = jnp.where(here & (field == 2), ref[0, r], tile)
+        tile = jnp.where(here & (field == 3), live, tile)
+    fz[z] = tile
+    wide[...] = jnp.zeros_like(wide)
+
+    pl.semaphore_wait(barrier, len(peers))
+
+    def remote(src, dst, send, recv, peer):
+        copy = pltpu.make_async_remote_copy(
+            src_ref=src, dst_ref=dst, send_sem=send, recv_sem=recv,
+            device_id=peer, device_id_type=MESH,
+        )
+        copy.start()
+        return copy
+
+    def spread(buf, own, send, recv, to):
+        return [
+            remote(buf.at[own], buf.at[own], send.at[j], recv.at[j], peer)
+            for j, peer in enumerate(to)
+        ]
+
+    def wait_all(copies):
+        for copy in copies:
+            copy.wait()
+
+    z_copies = []
+    for c, (k0, k1) in enumerate(bounds):
+        cols = pl.ds(k0, k1 - k0)
+        z_copies.append([
+            remote(hid.at[0, :, cols], zrows.at[z, :, cols], zs.at[c, j], zr.at[c, j], peer)
+            for j, peer in enumerate(z_peers)
+        ])
+        if c == 0:
+            f_z = spread(fz, z, fzs, fzr, z_peers)
+    zrows[z] = hid[0]
+
+    x_copies = []
+    for c, (k0, k1) in enumerate(bounds):
+        cols = pl.ds(k0, k1 - k0)
+        wait_all(z_copies[c])
+        for p in range(np_):
+            wide[p * slot_rows : p * slot_rows + local_rows, k0:k1] = zrows[p, :, k0:k1].astype(
+                jnp.float32
+            )
+        held[group, :, k0:k1] = wide[:, k0:k1].astype(held.dtype)
+        x_copies.append([
+            remote(
+                held.at[group, :, cols], held.at[group, :, cols], xs.at[c, j], xr.at[c, j], peer
+            )
+            for j, peer in enumerate(x_peers)
+        ])
+        if c == 0:
+            wait_all(f_z)
+            fx[group_own] = sum(fz[p] for p in range(np_))
+            f_x = spread(fx, group_own, fxs, fxr, x_peers)
+
+    def swap(c):
+        k0, k1 = bounds[c]
+        wait_all(x_copies[c])
+        view = held.at[pl.ds(lo * half, half), :, pl.ds(k0, k1 - k0)]
+        return remote(view, view, cs.at[c], cr.at[c], c_peer)
+
+    def product(rows, k0, k1):
+        rhs = held[:, :, k0:k1].reshape(lanes, k1 - k0)
+        return lax.dot_general(
+            wbuf[rows, k0:k1], rhs, (((1,), (1,)), ((), ())),
+            preferred_element_type=jnp.float32,
+        )
+
+    first_id = ((z * nv + y) * (ns * sub) + s * sub).astype(jnp.float32)
+    row_pos = lax.broadcasted_iota(jnp.int32, (block_rows, lanes), 0).astype(jnp.float32)
+    pending = swap(0)
+    carry = None
+    for c, (k0, k1) in enumerate(bounds):
+        pending.wait()
+        if c + 1 < len(bounds):
+            pending = swap(c + 1)
+        if c == 0:
+            for b in range(blocks):
+                w_copies[b].wait()
+                rows = pl.ds(b * block_rows, block_rows)
+                acc[rows, :] = product(rows, k0, k1)
+            wait_all(f_x)
+            fc[lo] = sum(fx[g] for g in range(half))
+            f_c = spread(fc, lo, fcs, fcr, [c_peer])
+        elif c + 1 < len(bounds):
+
+            @pl.loop(0, blocks)
+            def _(b):
+                rows = pl.ds(pl.multiple_of(b * block_rows, tile_rows), block_rows)
+                acc[rows, :] += product(rows, k0, k1)
+        else:
+            wait_all(f_c)
+            fields = fc[0] + fc[1]
+            wanted = fields[0:1] - first_id
+
+            def last(b, carry):
+                peak, total, target = carry
+                rows = pl.ds(pl.multiple_of(b * block_rows, tile_rows), block_rows)
+                logits = acc[rows, :] + product(rows, k0, k1)
+                shift = wanted - (b * block_rows).astype(jnp.float32)
+                hit = jnp.where(row_pos == shift, logits, 0.0).reshape(-1, 8, lanes)
+                cube = logits.reshape(-1, 8, lanes)
+                peak_new = jnp.maximum(peak, jnp.max(cube, axis=0))
+                total = total * jnp.exp(peak - peak_new) + jnp.sum(
+                    jnp.exp(cube - peak_new[None]), axis=0
+                )
+                return peak_new, total, target + jnp.sum(hit, axis=0)
+
+            start = (
+                jnp.full((8, lanes), -1e30, jnp.float32),
+                jnp.zeros((8, lanes), jnp.float32),
+                jnp.zeros((8, lanes), jnp.float32),
+            )
+            peak8, total8, target8 = lax.fori_loop(0, blocks, last, start)
+    peak = jnp.max(peak8, axis=0, keepdims=True)
+    total = jnp.sum(total8 * jnp.exp(peak8 - peak), axis=0, keepdims=True)
+    target = jnp.sum(target8, axis=0, keepdims=True)
+
+    def pack(peak, total, target):
+        return jnp.where(field == 0, peak, jnp.where(field == 1, total, target))
+
+    sc[lo] = pack(peak, total, target)
+    wait_all(spread(sc, lo, scs, scr, [c_peer]))
+    sx[group_own] = pack(*merge_slots([sc[g] for g in range(2)]))
+    wait_all(spread(sx, group_own, sxs, sxr, x_peers))
+    sz[z] = pack(*merge_slots([sx[g] for g in range(half)]))
+    wait_all(spread(sz, z, szs, szr, z_peers))
+    peak, total, target = merge_slots([sz[p] for p in range(np_)])
+
+    old_row, ref_row, live_row = fields[1:2], fields[2:3], fields[3:4] > 0.5
+    valid_row, score_row = fields[4:5], fields[5:6]
+
+    def over_samples(row):
+        row8 = jnp.broadcast_to(row, (8, lanes))
+        out = row8
+        for j in range(1, ns):
+            out = out + pltpu.roll(row8, j * nv * tile_rows, 1)
+        return out[0:1]
+
+    safe_count = jnp.maximum(over_samples(valid_row), 1.0)
+    group_mean = over_samples(valid_row * score_row) / safe_count
+    second = over_samples(valid_row * score_row * score_row) / safe_count
+    spread_row = jnp.sqrt(jnp.maximum(second - group_mean * group_mean, 0.0))
+    adv = valid_row * (score_row - group_mean) / jnp.maximum(spread_row, std_floor)
+    raw = target - (peak + jnp.log(total))
+    logp = jnp.where(live_row, raw, 0.0)
+    ratio = jnp.exp(raw - old_row)
+    gain = adv * jnp.minimum(ratio, clip_high)
+    down = jnp.maximum(adv * jnp.maximum(ratio, clip_low), dual_clip * adv)
+    objective = jnp.where(adv >= 0.0, gain, down)
+    gap = ref_row - raw
+    kl = jnp.exp(gap) - gap - 1.0
+    loss = jnp.where(live_row, kl_weight * kl - objective, 0.0)
+    loss_sum = jnp.sum(loss, axis=1, keepdims=True)
+    live_sum = jnp.sum(jnp.where(live_row, 1.0, 0.0), axis=1, keepdims=True)
+    mean_out[...] = loss_sum / jnp.maximum(live_sum, 1.0)
+
+    mixed = jnp.where(field == 0, logp, jnp.where(field == 1, loss, adv))
+    mine = pltpu.roll(mixed, lax.rem(lanes - base_lane, lanes), 1)
+    logp_out[...] = mine[0:1, 0:local_rows]
+    loss_out[...] = mine[1:2, 0:local_rows]
+    adv_out[...] = mine[2:3, 0:1]
+
+
+def local_fused(dims, *args):
+    np_, ns, nv, local_rows, slot_rows, sub, width, blocks = dims
+    half = ns // 2 * nv
+    n_chunks = len(chunk_bounds(width))
+    dma = pltpu.SemaphoreType.DMA
+    vmem = pl.BlockSpec(memory_space=pltpu.VMEM)
+    smem = pl.BlockSpec(memory_space=pltpu.SMEM)
+    tile = lambda n: pltpu.VMEM((n, 8, lanes), jnp.float32)
+    pair = lambda *shape: [dma(shape), dma(shape)]
+    outs = pl.pallas_call(
+        functools.partial(fused_kernel, dims),
+        out_shape=(
+            jax.ShapeDtypeStruct((1, local_rows), jnp.float32),
+            jax.ShapeDtypeStruct((1, local_rows), jnp.float32),
+            jax.ShapeDtypeStruct((1, 1), jnp.float32),
+            jax.ShapeDtypeStruct((1, 1), jnp.float32),
+        ),
+        in_specs=[vmem, pl.BlockSpec(memory_space=pl.ANY)] + [smem] * 7,
+        out_specs=(vmem,) * 4,
+        scratch_shapes=[
+            pltpu.VMEM((sub, width), jnp.bfloat16),
+            pltpu.VMEM((np_, local_rows, width), jnp.bfloat16),
+            pltpu.VMEM((tile_rows, width), jnp.float32),
+            pltpu.VMEM((2 * half, tile_rows, width), jnp.bfloat16),
+            pltpu.VMEM((sub, lanes), jnp.float32),
+            tile(np_), tile(half), tile(2), tile(np_), tile(half), tile(2),
+            dma((blocks,)),
+            *pair(n_chunks, np_ - 1), *pair(n_chunks, half - 1), *pair(n_chunks),
+            *pair(np_ - 1), *pair(half - 1), *pair(1),
+            *pair(np_ - 1), *pair(half - 1), *pair(1),
+        ],
+        compiler_params=pltpu.CompilerParams(
+            collective_id=0, has_side_effects=True, vmem_limit_bytes=60 * 1024 * 1024
+        ),
+    )(*args)
+    return outs[0], outs[1], outs[2], outs[3].reshape(())
+
+
+def local(hidden, unembed, *rest, shape):
+    np_, ns, nv = shape
+    samples, local_rows, width = hidden.shape
+    vocab_rows = unembed.shape[0]
+    slot_rows = tile_rows // np_ if tile_rows % np_ == 0 else 0
+    sub = vocab_rows // ns
+    blocks = row_blocks(sub)
+    fits = (
+        samples == 1
+        and rest[-1].shape == (1, 1)
+        and np_ > 1
+        and ns % 2 == 0
+        and ns // 2 * nv > 1
+        and ns * nv * tile_rows == lanes
+        and local_rows <= slot_rows
+        and vocab_rows % ns == 0
+        and blocks > 0
+        and width % 512 == 0
+        and width > 1024
+        and sub * (width * 2 + lanes * 4) <= 48 * 1024 * 1024
+    )
+    if not fits:
+        return local_plain(hidden, unembed, *rest)
+    dims = (np_, ns, nv, local_rows, slot_rows, sub, width, blocks)
+    return local_fused(dims, hidden, unembed, *rest)
+
+
 def solution(mesh):
     in_specs = (
         P("sample", ("prompt", "vocab"), None),
@@ -121,4 +440,6 @@
         P("prompt", "sample"),
         P(),
     )
-    return jax.shard_map(local, mesh=mesh, in_specs=in_specs, out_specs=out_specs, check_vma=False)
+    shape = (mesh.shape["prompt"], mesh.shape["sample"], mesh.shape["vocab"])
+    body = functools.partial(local, shape=shape)
+    return jax.shard_map(body, mesh=mesh, in_specs=in_specs, out_specs=out_specs, check_vma=False)

time: 174 us -> 48.7 us (0.28)
  blocking collectives: 109 us -> 0 us
  matrix products: 48 us -> 0 us
  Pallas kernels: 0 us -> 40.1 us
  other arithmetic: 3.97 us -> 0 us
  between operations: 9.57 us -> 6.07 us
    dot_general x1 -> x0, matrix products: 48 us -> none  [shard_stats(): lax.dot_general(row_block, weight, (((1,), (1,)), ((), ())), preferred_el...]
    psum x2 -> x0, blocking collectives: 47.6 us -> none  [the longest x1 37.1 us: local(): lax.psum((loss_part, jnp.sum(live_float)), ('prompt', 'sample', 'vocab'))]
    pallas_call x0 -> x1, Pallas kernels: none -> 40.1 us  [local_fused(): pl.pallas_call(functools.partial(fused_kernel, dims), out_shape=(jax.Shap...]
    all_gather x1 -> x0, blocking collectives: 31.5 us -> none  [local(): lax.all_gather(hidden, ('prompt', 'vocab'), axis=1, tiled=True)]
    unnamed x2 -> x0, blocking collectives: 29.7 us -> none
    reduce_sum x3 -> x0, other arithmetic: 3.27 us -> none  [the longest x1 1.35 us: local(): jnp.sum(live_float)]
where the time goes in v1:
time: 48.7 us; the launch traced here: 48.4 us
  Pallas kernels  40.1 us (82%)
  between operations  6.07 us (12%)
  local copies, waits for them, and re-layouts  2.25 us (5%)
    pallas_call x1, Pallas kernels, local_fused(): pl.pallas_call(functools.partial(fused_kernel, dims), out_shape=(jax.Shap...  40.1 us
    unnamed x2, local copies, waits for them, and re-layouts  2.25 us

profile of v1, /device:TPU:0, one launch (start us, length us, event | category | flops | bytes accessed | tf_op | source)
XLA Modules:
  0.0 48.4 jit_solution(397004231996878693)
XLA Ops:
  2.6 40.1 %shard_map.120 = (f32[1,3]{1,0:T(1,128)}, f32[1,3]{1,0:T(1,128)}, f32[1,1]{1,0:T(1,128)}, f32[1,1]{1,0:T(1,128)}) custom-call(bf16[1,3,3584]{2,1,0:T(4,128)(2,1)} %hid.1, bf16[19008,3584]{1,0:T(8,128)(2,1)} %weight.1, s32[1,3]{1,0:T(1,128)} %ids.1, f32[1,3]{1,0:T(1,128)} %old.1, f32[1,3]{1,0:T(1,128)} %ref.1, s32[1,3]{1,0:T(1,128)} %mask.1, ...), custom_call_target="tpu_custom_call" | custom-call | tf_op jit(solution)/shard_map/pallas_call | solution.py:369
  42.7 1.1 %copy.20 = f32[1,3]{1,0:T(1,128)} copy(f32[1,3]{1,0:T(1,128)} %get-tuple-element.16) | data formatting | bytes 24
  43.8 1.1 %copy.21 = f32[1,3]{1,0:T(1,128)} copy(f32[1,3]{1,0:T(1,128)} %get-tuple-element.17) | data formatting | bytes 24

commit v2 on v1

--- a/solution.py
+++ b/solution.py
@@ -138,9 +138,9 @@
 
 def fused_kernel(
     dims, hid, weight, ids, old, ref, mask, lengths, valid, rewards,
-    logp_out, loss_out, adv_out, mean_out,
-    wbuf, zrows, wide, held, acc, fz, fx, fc, sz, sx, sc,
-    wsem, zs, zr, xs, xr, cs, cr, fzs, fzr, fxs, fxr, fcs, fcr, szs, szr, sxs, sxr, scs, scr,
+    out,
+    wbuf, zrows, wide, held, acc, fz, fx, fc, sz, sx,
+    wsem, zs, zr, xs, xr, cs, cr, fzs, fzr, fxs, fxr, fcs, fcr, szs, szr, sxs, sxr,
 ):
     np_, ns, nv, local_rows, slot_rows, sub, width, blocks = dims
     hi_count = ns // 2
@@ -167,7 +167,9 @@
     x_peers = [(z, lax.rem(hi + a, hi_count) * 2 + lo, lax.rem(y + b, nv)) for a, b in plane]
     c_peer = (z, hi * 2 + (1 - lo), y)
     barrier = pltpu.get_barrier_semaphore()
-    peers = z_peers + x_peers + [c_peer]
+    far_peers = [(pz, ps + 1 - 2 * lo, py) for pz, ps, py in x_peers]
+    block_peers = [c_peer] + x_peers + far_peers
+    peers = z_peers + block_peers
     for peer in peers:
         pl.semaphore_signal(barrier, inc=1, device_id=peer, device_id_type=MESH)
 
@@ -267,10 +269,10 @@
     carry = None
     for c, (k0, k1) in enumerate(bounds):
         pending.wait()
-        if c + 1 < len(bounds):
-            pending = swap(c + 1)
         if c == 0:
             for b in range(blocks):
+                if b == blocks // 2:
+                    pending = swap(1)
                 w_copies[b].wait()
                 rows = pl.ds(b * block_rows, block_rows)
                 acc[rows, :] = product(rows, k0, k1)
@@ -279,10 +281,13 @@
             f_c = spread(fc, lo, fcs, fcr, [c_peer])
         elif c + 1 < len(bounds):
 
-            @pl.loop(0, blocks)
-            def _(b):
+            def middle(b):
                 rows = pl.ds(pl.multiple_of(b * block_rows, tile_rows), block_rows)
                 acc[rows, :] += product(rows, k0, k1)
+
+            pl.loop(0, blocks // 2)(middle)
+            pending = swap(c + 1)
+            pl.loop(blocks // 2, blocks)(middle)
         else:
             wait_all(f_c)
             fields = fc[0] + fc[1]
@@ -314,11 +319,9 @@
     def pack(peak, total, target):
         return jnp.where(field == 0, peak, jnp.where(field == 1, total, target))
 
-    sc[lo] = pack(peak, total, target)
-    wait_all(spread(sc, lo, scs, scr, [c_peer]))
-    sx[group_own] = pack(*merge_slots([sc[g] for g in range(2)]))
-    wait_all(spread(sx, group_own, sxs, sxr, x_peers))
-    sz[z] = pack(*merge_slots([sx[g] for g in range(half)]))
+    sx[group] = pack(peak, total, target)
+    wait_all(spread(sx, group, sxs, sxr, block_peers))
+    sz[z] = pack(*merge_slots([sx[g] for g in range(2 * half)]))
     wait_all(spread(sz, z, szs, szr, z_peers))
     peak, total, target = merge_slots([sz[p] for p in range(np_)])
 
@@ -327,10 +330,10 @@
 
     def over_samples(row):
         row8 = jnp.broadcast_to(row, (8, lanes))
-        out = row8
+        summed = row8
         for j in range(1, ns):
-            out = out + pltpu.roll(row8, j * nv * tile_rows, 1)
-        return out[0:1]
+            summed = summed + pltpu.roll(row8, j * nv * tile_rows, 1)
+        return summed[0:1]
 
     safe_count = jnp.maximum(over_samples(valid_row), 1.0)
     group_mean = over_samples(valid_row * score_row) / safe_count
@@ -348,13 +351,11 @@
     loss = jnp.where(live_row, kl_weight * kl - objective, 0.0)
     loss_sum = jnp.sum(loss, axis=1, keepdims=True)
     live_sum = jnp.sum(jnp.where(live_row, 1.0, 0.0), axis=1, keepdims=True)
-    mean_out[...] = loss_sum / jnp.maximum(live_sum, 1.0)
+    mean = loss_sum / jnp.maximum(live_sum, 1.0)
 
     mixed = jnp.where(field == 0, logp, jnp.where(field == 1, loss, adv))
     mine = pltpu.roll(mixed, lax.rem(lanes - base_lane, lanes), 1)
-    logp_out[...] = mine[0:1, 0:local_rows]
-    loss_out[...] = mine[1:2, 0:local_rows]
-    adv_out[...] = mine[2:3, 0:1]
+    out[...] = jnp.where(field == 3, mean, mine)
 
 
 def local_fused(dims, *args):
@@ -366,33 +367,28 @@
     smem = pl.BlockSpec(memory_space=pltpu.SMEM)
     tile = lambda n: pltpu.VMEM((n, 8, lanes), jnp.float32)
     pair = lambda *shape: [dma(shape), dma(shape)]
-    outs = pl.pallas_call(
+    out = pl.pallas_call(
         functools.partial(fused_kernel, dims),
-        out_shape=(
-            jax.ShapeDtypeStruct((1, local_rows), jnp.float32),
-            jax.ShapeDtypeStruct((1, local_rows), jnp.float32),
-            jax.ShapeDtypeStruct((1, 1), jnp.float32),
-            jax.ShapeDtypeStruct((1, 1), jnp.float32),
-        ),
+        out_shape=jax.ShapeDtypeStruct((8, lanes), jnp.float32),
         in_specs=[vmem, pl.BlockSpec(memory_space=pl.ANY)] + [smem] * 7,
-        out_specs=(vmem,) * 4,
+        out_specs=vmem,
         scratch_shapes=[
             pltpu.VMEM((sub, width), jnp.bfloat16),
             pltpu.VMEM((np_, local_rows, width), jnp.bfloat16),
             pltpu.VMEM((tile_rows, width), jnp.float32),
             pltpu.VMEM((2 * half, tile_rows, width), jnp.bfloat16),
             pltpu.VMEM((sub, lanes), jnp.float32),
-            tile(np_), tile(half), tile(2), tile(np_), tile(half), tile(2),
+            tile(np_), tile(half), tile(2), tile(np_), tile(2 * half),
             dma((blocks,)),
             *pair(n_chunks, np_ - 1), *pair(n_chunks, half - 1), *pair(n_chunks),
             *pair(np_ - 1), *pair(half - 1), *pair(1),
-            *pair(np_ - 1), *pair(half - 1), *pair(1),
+            *pair(np_ - 1), *pair(2 * half - 1),
         ],
         compiler_params=pltpu.CompilerParams(
             collective_id=0, has_side_effects=True, vmem_limit_bytes=60 * 1024 * 1024
         ),
     )(*args)
-    return outs[0], outs[1], outs[2], outs[3].reshape(())
+    return out[0:1, :local_rows], out[1:2, :local_rows], out[2:3, :1], out[3, 0]
 
 
 def local(hidden, unembed, *rest, shape):

time: 48.7 us -> 44.6 us (0.916)
  between operations: 6.07 us -> 2.58 us
  Pallas kernels: 40.1 us -> 39.2 us
    slice x0 -> x2, local copies, waits for them, and re-layouts: none -> 2.53 us  [the longest x1 1.26 us: local_fused(): out[3, 0]]
    unnamed x2 -> x0, local copies, waits for them, and re-layouts: 2.25 us -> none
    pallas_call x1, Pallas kernels: 40.1 us -> 39.2 us  [local_fused(): pl.pallas_call(functools.partial(fused_kernel, dims), out_shape=jax.Shape...]
where the time goes in v2:
time: 44.6 us; the launch traced here: 44.3 us
  Pallas kernels  39.2 us (88%)
  between operations  2.58 us (6%)
  local copies, waits for them, and re-layouts  2.53 us (6%)
    pallas_call x1, Pallas kernels, local_fused(): pl.pallas_call(functools.partial(fused_kernel, dims), out_shape=jax.Shape...  39.2 us
    slice x1, local copies, waits for them, and re-layouts, local_fused(): out[3, 0]  1.26 us
    slice x1, local copies, waits for them, and re-layouts, local_fused(): out[1:2, :local_rows]  1.26 us

profile of v2, /device:TPU:0, one launch (start us, length us, event | category | flops | bytes accessed | tf_op | source)
XLA Modules:
  0.0 44.3 jit_solution(7746703180738196170)
XLA Ops:
  2.6 39.2 %shard_map.120 = f32[8,128]{1,0:T(8,128)} custom-call(bf16[1,3,3584]{2,1,0:T(4,128)(2,1)} %hid.1, bf16[19008,3584]{1,0:T(8,128)(2,1)} %weight.1, s32[1,3]{1,0:T(1,128)} %ids.1, f32[1,3]{1,0:T(1,128)} %old.1, f32[1,3]{1,0:T(1,128)} %ref.1, s32[1,3]{1,0:T(1,128)} %mask.1, s32[1,1]{1,0:T(1,128)S(6)} %copy.13.lengths, s32[1,1]{1,0:T(1,128)S(6)} %copy.14.valid, ...), custom_call_target="tpu_custom_call" | custom-call | tf_op jit(solution)/shard_map/pallas_call | solution.py:370
  41.7 1.3 %fusion = (f32[1,1]{1,0:T(1,128)}, f32[1,1]{1,0:T(1,128)}) fusion(f32[8,128]{1,0:T(8,128)} %shard_map.120), kind=kLoop, calls=%fused_computation | loop fusion | bytes 16 | tf_op jit(solution)/shard_map/slice | solution.py:391
  43.0 1.3 %fusion.1 = (f32[1,3]{1,0:T(1,128)}, f32[1,3]{1,0:T(1,128)}) fusion(f32[8,128]{1,0:T(8,128)} %shard_map.120), kind=kLoop, calls=%fused_computation.1 | loop fusion | bytes 48 | tf_op jit(solution)/shard_map/slice | solution.py:391
